TPU v7x, 32 devices: a whole 2x2x4 slice. The times are simulated.
32 devices in a mesh: ctx: 8 (over y, x, core), tp: 4 (over z).
Axes of the slice: x: 2, y: 2, z: 4, core: 2. Of those that a mesh axis runs over, the one named last changes fastest.
Arguments:
- hidden: bfloat16 [8, 8192], P(None, 'ctx'), may hold values from -4.8 to 4.8, as said below
- norm_gains: bfloat16 [4, 8192], P(None, 'ctx'), may hold values from 0.5 to 1.5
- w_query: bfloat16 [4, 8192, 8192], P(None, 'ctx', 'tp'), may hold values from -0.0625 to 0.0625
- w_key: bfloat16 [4, 8192, 1024], P(None, 'ctx', 'tp'), may hold values from -0.125 to 0.125
- w_value: bfloat16 [4, 8192, 1024], P(None, 'ctx', 'tp'), may hold values from -0.125 to 0.125
- w_out: bfloat16 [4, 8192, 8192], P(None, 'tp', 'ctx'), may hold values from -0.0625 to 0.0625
- key_cache: bfloat16 [4, 8, 8, 1024, 128], P(None, None, 'tp', 'ctx'), may hold values from -9 to 9
- value_cache: bfloat16 [4, 8, 8, 1024, 128], P(None, None, 'tp', 'ctx'), may hold values from -6 to 6
- lengths: int32 [8], replicated, may hold values from 1 to 1024, 4104 in all
Outputs:
- updated: float32 [8, 8192], P(None, 'ctx')
Inputs may be any that keep to these rules, and one draw needn't show every extreme that they name: Each sequence has lengths[b] valid cache positions 0 .. lengths[b] - 1, between 1 and 1024; the longest sequence has exactly 1024; the new token sits at position lengths[b]. `hidden`: activations of order 0.2; in each block of 1024 consecutive features one sequence, chosen at random, has entries four times larger.
All inputs are finite; a program needn't handle non-finite values.
Results may differ from a plain program's by a relative error of at most 0.02.
Values sent between devices are 32-bit elements.
A program may use at most 128 MiB of HBM per device.

v0:
```python
import math

import jax
import jax.numpy as jnp
from jax import lax
from jax.sharding import PartitionSpec as P

D = 8192


mask_fill = -1e30
norm_eps = 1e-05
rope_base = 500000.0


def merged(value, axis, join):
    pieces = jax.tree.map(lambda part: lax.all_gather(part, axis), value)
    head = jax.tree.map(lambda part: part[0], pieces)
    tail = jax.tree.map(lambda part: part[1:], pieces)
    total, _ = lax.scan(lambda total, slab: (join(total, slab), None), head, tail)
    return total


def rotate(vectors, positions):
    width = vectors.shape[-1]
    half_width = width // 2
    exponents = jnp.arange(half_width, dtype=jnp.float32) * (2.0 / width)
    frequency = jnp.exp(-exponents * math.log(rope_base))
    angles = positions.astype(jnp.float32)[:, None] * frequency[None, :]
    cosine = jnp.cos(angles)[:, None, :]
    sine_part = jnp.sin(angles)[:, None, :]
    first_half = vectors[..., :half_width]
    second_half = vectors[..., half_width:]
    return jnp.concatenate(
        [
            first_half * cosine - second_half * sine_part,
            second_half * cosine + first_half * sine_part,
        ],
        axis=-1,
    )


def combine_partial(one_side, other_side):
    first_max, first_sum, first_out = one_side
    second_max, second_sum, second_out = other_side
    largest = jnp.maximum(first_max, second_max)
    first_factor = jnp.exp(first_max - largest)
    second_factor = jnp.exp(second_max - largest)
    merged_sum = first_sum * first_factor + second_sum * second_factor
    merged_out = first_out * first_factor[..., None] + second_out * second_factor[..., None]
    return (largest, merged_sum, merged_out)


def shards(hidden, norm_gains, w_query, w_key, w_value, w_out, key_cache, value_cache, lengths):
    stream = hidden.astype(jnp.float32)
    seq_count = hidden.shape[0]
    head_width = key_cache.shape[4]
    location_total = key_cache.shape[3]
    kv_local = key_cache.shape[2]
    query_local = w_query.shape[2] // head_width
    group_size = query_local // kv_local
    logit_multiplier = 1.0 / math.sqrt(head_width)
    positions = lax.axis_index("ctx") * location_total + jnp.arange(location_total, dtype=jnp.int32)
    usable = (positions[None, :] < lengths[:, None])[:, None, None, :]
    for layer_idx in range(w_query.shape[0]):
        local_squares = jnp.sum(stream * stream, axis=1)
        scaled = (stream * norm_gains[layer_idx].astype(jnp.float32)).astype(jnp.bfloat16)
        query_part = jnp.dot(scaled, w_query[layer_idx], preferred_element_type=jnp.float32)
        key_part = jnp.dot(scaled, w_key[layer_idx], preferred_element_type=jnp.float32)
        value_part = jnp.dot(scaled, w_value[layer_idx], preferred_element_type=jnp.float32)
        squares = lax.psum(local_squares, "ctx")
        raw_query, raw_key, raw_value = lax.psum((query_part, key_part, value_part), "ctx")
        reciprocal_value = lax.rsqrt(squares / D + norm_eps)
        query = rotate(
            (raw_query * reciprocal_value[:, None]).reshape(seq_count, query_local, head_width),
            lengths,
        ).astype(jnp.bfloat16)
        fresh_lookup_vector = rotate(
            (raw_key * reciprocal_value[:, None]).reshape(seq_count, kv_local, head_width), lengths
        ).astype(jnp.bfloat16)
        new_value = (
            (raw_value * reciprocal_value[:, None])
            .reshape(seq_count, kv_local, head_width)
            .astype(jnp.bfloat16)
        )
        shared_head_sets = query.reshape(seq_count, kv_local, group_size, head_width)
        scores = (
            jnp.einsum(
                "bkgd,bksd->bkgs",
                shared_head_sets,
                key_cache[layer_idx],
                preferred_element_type=jnp.float32,
            )
            * logit_multiplier
        )
        masked = jnp.where(usable, scores, mask_fill)
        local_max = jnp.max(masked, axis=-1)
        attention_probabilities = jnp.where(usable, jnp.exp(masked - local_max[..., None]), 0.0)
        local_sum = jnp.sum(attention_probabilities, axis=-1)
        local_out = jnp.einsum(
            "bkgs,bksd->bkgd",
            attention_probabilities.astype(jnp.bfloat16),
            value_cache[layer_idx],
            preferred_element_type=jnp.float32,
        )
        largest, total_sum, total_out = merged(
            (local_max, local_sum, local_out), "ctx", combine_partial
        )
        self_match_logit = (
            jnp.einsum(
                "uryj,urj->ury",
                shared_head_sets,
                fresh_lookup_vector,
                preferred_element_type=jnp.float32,
            )
            * logit_multiplier
        )
        row_top = jnp.maximum(largest, self_match_logit)
        carried = jnp.exp(largest - row_top)
        fresh = jnp.exp(self_match_logit - row_top)
        fresh_rounded = lax.optimization_barrier(fresh.astype(jnp.bfloat16)).astype(jnp.float32)
        numerator = (
            total_out * carried[..., None]
            + fresh_rounded[..., None] * new_value.astype(jnp.float32)[:, :, None, :]
        )
        denominator = total_sum * carried + fresh
        context = (
            (numerator / denominator[..., None])
            .reshape(seq_count, query_local * head_width)
            .astype(jnp.bfloat16)
        )
        head_part = jnp.dot(context, w_out[layer_idx], preferred_element_type=jnp.float32)
        stream = stream + lax.psum(head_part, "tp")
    return stream


def solution(mesh):
    return jax.shard_map(
        shards,
        mesh=mesh,
        in_specs=(
            P(None, "ctx"),
            P(None, "ctx"),
            P(None, "ctx", "tp"),
            P(None, "ctx", "tp"),
            P(None, "ctx", "tp"),
            P(None, "tp", "ctx"),
            P(None, None, "tp", "ctx", None),
            P(None, None, "tp", "ctx", None),
            P(),
        ),
        out_specs=P(None, "ctx"),
        check_vma=False,
    )
```

profile of v0, /device:TPU:0, one launch (start us, length us, event | category | flops | bytes accessed | tf_op | source)
XLA Modules:
  0.0 525.5 jit_solution(14332039399861125533)
XLA Ops:
  7.4 3.6 fusion.30
  11.5 1.2 fusion.67
  12.7 25.6 %all-reduce.3 = (f32[8]{0:T(128)S(1)}, f32[8,256]{1,0:T(8,128)S(1)}, f32[8,256]{1,0:T(8,128)S(1)}) all-reduce(f32[8]{0:T(128)S(1)} %fusion.97, f32[8,256]{1,0:T(8,128)S(1)} %fusion.67, f32[8,256]{1,0:T(8,128)S(1)} %fusion.65), channel_id=1, replica_groups=mesh['ctx'=8,'tp'=4] {'ctx'}, use_global_device_ids=true, to_apply=%region_2.0 | all-reduce | flops 4104 | bytes 32832 | tf_op jit(solution)/shard_map/psum | solution.py:71
  38.7 28.5 %all-reduce.9.cloned.1.call-done = f32[8,2048]{1,0:T(8,128)} async-done(((f32[8,2048]{1,0:T(8,128)}), f32[8,2048]{1,0:T(8,128)}) %all-reduce.9.cloned.1.call-update) | async-done | bytes 65552 | tf_op jit(solution)/shard_map/psum | solution.py:72
  68.3 1.5 fusion.175
  69.8 1.4 fusion.69
  71.1 9.2 %all-gather.2 = f32[64,2,8,128]{3,2,1,0:T(8,128)S(1)} all-gather(f32[8,2,8,128]{3,2,1,0:T(8,128)S(1)} %fusion.69), channel_id=4, replica_groups=mesh['ctx'=8,'tp'=4] {'ctx'}, dimensions={0}, use_global_device_ids=true | all-gather | bytes 589824 | tf_op jit(solution)/shard_map/all_gather | solution.py:17
  80.6 8.8 %all-gather.1 = f32[64,2,8]{2,1,0:T(2,128)S(1)} all-gather(f32[8,2,8]{2,1,0:T(2,128)S(1)} %fusion.89), channel_id=3, replica_groups=mesh['ctx'=8,'tp'=4] {'ctx'}, dimensions={0}, use_global_device_ids=true | all-gather | bytes 4608 | tf_op jit(solution)/shard_map/all_gather | solution.py:17
  89.4 8.5 %all-gather = f32[64,2,8]{2,1,0:T(2,128)S(1)} all-gather(f32[8,2,8]{2,1,0:T(2,128)S(1)} %get-tuple-element.397), channel_id=2, replica_groups=mesh['ctx'=8,'tp'=4] {'ctx'}, dimensions={0}, use_global_device_ids=true | all-gather | bytes 4608 | tf_op jit(solution)/shard_map/all_gather | solution.py:17
  98.0 1.4 while.56
  99.8 2.8 fusion.28
  102.6 19.0 %psum.144 = f32[8,1024]{1,0:T(8,128)S(1)} all-reduce(f32[8,1024]{1,0:T(8,128)S(1)} %fusion.28), channel_id=1, replica_groups=mesh['ctx'=8,'tp'=4] {'tp'}, use_global_device_ids=true, to_apply=%region_9.10 | all-reduce | flops 8192 | bytes 65536 | tf_op jit(solution)/shard_map/psum | solution.py:133
  121.9 1.2 fusion.60
  123.1 3.5 fusion.26
  126.6 22.3 %all-reduce.2 = (f32[8]{0:T(128)S(1)}, f32[8,256]{1,0:T(8,128)S(1)}, f32[8,256]{1,0:T(8,128)S(1)}) all-reduce(f32[8]{0:T(128)S(1)} %get-tuple-element.361, f32[8,256]{1,0:T(8,128)S(1)} %fusion.60, f32[8,256]{1,0:T(8,128)S(1)} %fusion.58), channel_id=1, replica_groups=mesh['ctx'=8,'tp'=4] {'ctx'}, use_global_device_ids=true, to_apply=%region_12.13 | all-reduce | flops 4104 | bytes 32832 | tf_op jit(solution)/shard_map/psum | solution.py:71
  149.3 50.2 %all-reduce.11.cloned.1.call-done = f32[8,2048]{1,0:T(8,128)} async-done(((f32[8,2048]{1,0:T(8,128)}), f32[8,2048]{1,0:T(8,128)}) %all-reduce.11.cloned.1.call-update) | async-done | bytes 65552 | tf_op jit(solution)/shard_map/psum | solution.py:72
  200.5 1.5 fusion.176
  202.0 1.4 fusion.62
  203.4 9.2 %all-gather.5 = f32[64,2,8,128]{3,2,1,0:T(8,128)S(1)} all-gather(f32[8,2,8,128]{3,2,1,0:T(8,128)S(1)} %fusion.62), channel_id=7, replica_groups=mesh['ctx'=8,'tp'=4] {'ctx'}, dimensions={0}, use_global_device_ids=true | all-gather | bytes 589824 | tf_op jit(solution)/shard_map/all_gather | solution.py:17
  212.8 8.8 %all-gather.4 = f32[64,2,8]{2,1,0:T(2,128)S(1)} all-gather(f32[8,2,8]{2,1,0:T(2,128)S(1)} %fusion.91), channel_id=6, replica_groups=mesh['ctx'=8,'tp'=4] {'ctx'}, dimensions={0}, use_global_device_ids=true | all-gather | bytes 4608 | tf_op jit(solution)/shard_map/all_gather | solution.py:17
  221.6 8.5 %all-gather.3 = f32[64,2,8]{2,1,0:T(2,128)S(1)} all-gather(f32[8,2,8]{2,1,0:T(2,128)S(1)} %get-tuple-element.399), channel_id=5, replica_groups=mesh['ctx'=8,'tp'=4] {'ctx'}, dimensions={0}, use_global_device_ids=true | all-gather | bytes 4608 | tf_op jit(solution)/shard_map/all_gather | solution.py:17
  230.4 1.4 while.57
  231.9 2.8 fusion.24
  234.8 19.0 %psum.149 = f32[8,1024]{1,0:T(8,128)S(1)} all-reduce(f32[8,1024]{1,0:T(8,128)S(1)} %fusion.24), channel_id=1, replica_groups=mesh['ctx'=8,'tp'=4] {'tp'}, use_global_device_ids=true, to_apply=%region_19.20 | all-reduce | flops 8192 | bytes 65536 | tf_op jit(solution)/shard_map/psum | solution.py:133
  254.1 1.2 fusion.53
  255.3 3.5 fusion.22
  258.8 22.3 %all-reduce.1 = (f32[8]{0:T(128)S(1)}, f32[8,256]{1,0:T(8,128)S(1)}, f32[8,256]{1,0:T(8,128)S(1)}) all-reduce(f32[8]{0:T(128)S(1)} %get-tuple-element.343, f32[8,256]{1,0:T(8,128)S(1)} %fusion.53, f32[8,256]{1,0:T(8,128)S(1)} %fusion.51), channel_id=1, replica_groups=mesh['ctx'=8,'tp'=4] {'ctx'}, use_global_device_ids=true, to_apply=%region_22.23 | all-reduce | flops 4104 | bytes 32832 | tf_op jit(solution)/shard_map/psum | solution.py:71
  281.5 50.2 %all-reduce.13.cloned.1.call-done = f32[8,2048]{1,0:T(8,128)} async-done(((f32[8,2048]{1,0:T(8,128)}), f32[8,2048]{1,0:T(8,128)}) %all-reduce.13.cloned.1.call-update) | async-done | bytes 65552 | tf_op jit(solution)/shard_map/psum | solution.py:72
  332.7 1.5 fusion.177
  334.2 1.4 fusion.55
  335.6 9.4 %all-gather.8 = f32[64,2,8,128]{3,2,1,0:T(8,128)S(1)} all-gather(f32[8,2,8,128]{3,2,1,0:T(8,128)S(1)} %fusion.55), channel_id=10, replica_groups=mesh['ctx'=8,'tp'=4] {'ctx'}, dimensions={0}, use_global_device_ids=true | all-gather | bytes 589824 | tf_op jit(solution)/shard_map/all_gather | solution.py:17
  345.2 8.8 %all-gather.7 = f32[64,2,8]{2,1,0:T(2,128)S(1)} all-gather(f32[8,2,8]{2,1,0:T(2,128)S(1)} %fusion.93), channel_id=9, replica_groups=mesh['ctx'=8,'tp'=4] {'ctx'}, dimensions={0}, use_global_device_ids=true | all-gather | bytes 4608 | tf_op jit(solution)/shard_map/all_gather | solution.py:17
  354.0 8.5 %all-gather.6 = f32[64,2,8]{2,1,0:T(2,128)S(1)} all-gather(f32[8,2,8]{2,1,0:T(2,128)S(1)} %get-tuple-element.401), channel_id=8, replica_groups=mesh['ctx'=8,'tp'=4] {'ctx'}, dimensions={0}, use_global_device_ids=true | all-gather | bytes 4608 | tf_op jit(solution)/shard_map/all_gather | solution.py:17
  362.7 1.4 while.58
  364.3 2.8 fusion.20
  367.2 19.0 %psum.154 = f32[8,1024]{1,0:T(8,128)S(1)} all-reduce(f32[8,1024]{1,0:T(8,128)S(1)} %fusion.20), channel_id=1, replica_groups=mesh['ctx'=8,'tp'=4] {'tp'}, use_global_device_ids=true, to_apply=%region_29.30 | all-reduce | flops 8192 | bytes 65536 | tf_op jit(solution)/shard_map/psum | solution.py:133
  386.5 1.2 fusion.46
  387.7 3.5 fusion.18
  391.2 22.3 %all-reduce = (f32[8]{0:T(128)S(1)}, f32[8,256]{1,0:T(8,128)S(1)}, f32[8,256]{1,0:T(8,128)S(1)}) all-reduce(f32[8]{0:T(128)S(1)} %get-tuple-element.341, f32[8,256]{1,0:T(8,128)S(1)} %fusion.46, f32[8,256]{1,0:T(8,128)S(1)} %fusion.44), channel_id=1, replica_groups=mesh['ctx'=8,'tp'=4] {'ctx'}, use_global_device_ids=true, to_apply=%region_32.33 | all-reduce | flops 4104 | bytes 32832 | tf_op jit(solution)/shard_map/psum | solution.py:71
  413.8 50.2 %all-reduce.15.cloned.1.call-done = f32[8,2048]{1,0:T(8,128)} async-done(((f32[8,2048]{1,0:T(8,128)}), f32[8,2048]{1,0:T(8,128)}) %all-reduce.15.cloned.1.call-update) | async-done | bytes 65552 | tf_op jit(solution)/shard_map/psum | solution.py:72
  465.0 1.5 fusion.178
  466.6 1.4 fusion.48
  467.9 9.2 %all-gather.11 = f32[64,2,8,128]{3,2,1,0:T(8,128)S(1)} all-gather(f32[8,2,8,128]{3,2,1,0:T(8,128)S(1)} %fusion.48), channel_id=13, replica_groups=mesh['ctx'=8,'tp'=4] {'ctx'}, dimensions={0}, use_global_device_ids=true | all-gather | bytes 589824 | tf_op jit(solution)/shard_map/all_gather | solution.py:17
  477.4 8.8 %all-gather.10 = f32[64,2,8]{2,1,0:T(2,128)S(1)} all-gather(f32[8,2,8]{2,1,0:T(2,128)S(1)} %fusion.95), channel_id=12, replica_groups=mesh['ctx'=8,'tp'=4] {'ctx'}, dimensions={0}, use_global_device_ids=true | all-gather | bytes 4608 | tf_op jit(solution)/shard_map/all_gather | solution.py:17
  486.2 8.5 %all-gather.9 = f32[64,2,8]{2,1,0:T(2,128)S(1)} all-gather(f32[8,2,8]{2,1,0:T(2,128)S(1)} %get-tuple-element.403), channel_id=11, replica_groups=mesh['ctx'=8,'tp'=4] {'ctx'}, dimensions={0}, use_global_device_ids=true | all-gather | bytes 4608 | tf_op jit(solution)/shard_map/all_gather | solution.py:17
  494.9 1.4 while.59
  496.5 2.8 fusion.16
  499.4 19.0 %psum.159 = f32[8,1024]{1,0:T(8,128)S(1)} all-reduce(f32[8,1024]{1,0:T(8,128)S(1)} %fusion.16), channel_id=1, replica_groups=mesh['ctx'=8,'tp'=4] {'tp'}, use_global_device_ids=true, to_apply=%region_39.40 | all-reduce | flops 8192 | bytes 65536 | tf_op jit(solution)/shard_map/psum | solution.py:133
  (266 shorter events, 14.6 us)
Async XLA Ops:
  6.5 60.7 %all-reduce.9.cloned.1.call-start = ((), (), s32[]{:S(2)}) async-start(), calls=%async_computation | async-start | bytes 131072 | tf_op jit(solution)/shard_map/psum | solution.py:72
  7.4 3.7 copy-start.1
  7.4 3.9 copy-start
  7.4 30.8 %copy-start.2 = (s32[8]{0:T(128)S(1)}, s32[8]{0:T(128)}, u32[]{:S(2)}) copy-start(s32[8]{0:T(128)} %param.25) | copy-start | bytes 100
  11.1 188.3 %all-reduce.11.cloned.1.call-start = ((), (), s32[]{:S(2)}) async-start(), calls=%async_computation.1 | async-start | bytes 131072 | tf_op jit(solution)/shard_map/psum | solution.py:72
  149.1 182.5 %all-reduce.13.cloned.1.call-start = ((), (), s32[]{:S(2)}) async-start(), calls=%async_computation.2 | async-start | bytes 131072 | tf_op jit(solution)/shard_map/psum | solution.py:72
  281.3 182.7 %all-reduce.15.cloned.1.call-start = ((), (), s32[]{:S(2)}) async-start(), calls=%async_computation.3 | async-start | bytes 131072 | tf_op jit(solution)/shard_map/psum | solution.py:72
Sparse Core Ops, SparseCore 0:
  11.2 55.9 all-reduce.8
  149.2 50.1 all-reduce.10
  281.4 50.1 all-reduce.12
  413.8 50.1 all-reduce.14
where the time goes:
time: 527 us; the launch traced here: 525 us
  blocking collectives  275 us (52%)
  waiting for transfers between devices  179 us (34%)
  matrix products  43.4 us (8%)
  between operations  13.6 us (3%)
  other arithmetic  12 us (2%)
    psum x4, waiting for transfers between devices, shards(): lax.psum((query_part, key_part, value_part), 'ctx')  179 us
    all_gather x12, blocking collectives, merged(): pieces = jax.tree.map(lambda part: lax.all_gather(part, axis), value)  106 us
    psum x4, blocking collectives, shards(): squares = lax.psum(local_squares, 'ctx')  92.6 us
    psum x4, blocking collectives, shards(): stream = stream + lax.psum(head_part, 'tp')  75.9 us
    dot_general x4, matrix products, shards(): jnp.dot(scaled, w_query[layer_idx], preferred_element_type=jnp.float32)  14 us
    dot_general x4, matrix products, shards(): jnp.dot(context, w_out[layer_idx], preferred_element_type=jnp.float32)  11.4 us
  transfers between devices with their start and end apart: 4, of which 4 were waited for; matrix products, arithmetic and copies ran while one was open for 0% of the time, Pallas kernels for 0%

commit v1 on v0

v1 whole, which is shorter than its diff:
```python
import functools
import math

import jax
import jax.numpy as jnp
from jax import lax
from jax.experimental import pallas as pl
from jax.experimental.pallas import tpu as pltpu
from jax.sharding import PartitionSpec as P

mask_fill = -1e30
norm_eps = 1e-05
rope_base = 500000.0
MESH = pl.DeviceIdType.MESH


def kernel(dims, hidden_ref, gains_ref, lengths_ref, wq_h, wk_h, wv_h, wo_h, kc_h, vc_h, out_ref,
           wq, wk, wv, wo, kc, vc, gain, bias, cosine, sine, qp, qr, kvp, kvr, qf, qown, otmp, stmp,
           op, orr, cf, tps, tpr, w_sem, s_sem, r_sem, ts_sem, tr_sem):
    n, tn, layers, batch, feat, total, heads, kvl, hd, span = dims
    group = heads // kvl
    hpo = max(1, heads // n)
    owners = heads // hpo
    f32, bf16 = jnp.float32, jnp.bfloat16
    scale = 1.0 / math.sqrt(hd)
    me = lax.axis_index("ctx")
    mt = lax.axis_index("tp")
    weights = ((wq_h, wq), (wk_h, wk), (wv_h, wv), (kc_h, kc), (vc_h, vc), (wo_h, wo))

    def load(index, layer):
        source, target = weights[index]
        return pltpu.make_async_copy(source.at[layer], target.at[layer], w_sem.at[index, layer])

    for index in range(len(weights)):
        load(index, 0).start()

    peers = [lax.rem(me + r, n) for r in range(1, n)]
    tpeers = [lax.rem(mt + r, tn) for r in range(1, tn)]
    barrier = pltpu.get_barrier_semaphore()
    for p in peers:
        pl.semaphore_signal(barrier, inc=1, device_id={"ctx": p}, device_id_type=MESH)
    for p in tpeers:
        pl.semaphore_signal(barrier, inc=1, device_id={"tp": p}, device_id_type=MESH)

    row = lax.broadcasted_iota(jnp.int32, (batch, hd), 0)
    lane = lax.broadcasted_iota(jnp.int32, (batch, hd), 1)
    times = jnp.zeros((batch, hd), jnp.int32)
    slot = lax.broadcasted_iota(jnp.int32, (heads, span), 1) + me * span
    for b in range(batch):
        times = jnp.where(row == b, lengths_ref[b], times)
        bias[b * heads:(b + 1) * heads, :] = jnp.where(slot < lengths_ref[b], 0.0, mask_fill)
    half = hd // 2
    low = lane < half
    exponent = jnp.where(low, lane, lane - half).astype(f32) * (2.0 / hd)
    angle = times.astype(f32) * jnp.exp(-exponent * math.log(rope_base))
    cosine[...] = jnp.cos(angle)
    sine[...] = jnp.where(low, -jnp.sin(angle), jnp.sin(angle))
    for l in range(layers):
        gain[l] = jnp.broadcast_to(gains_ref[l:l + 1, :].astype(f32), (batch, feat))
    out_ref[...] = hidden_ref[...].astype(f32)

    pl.semaphore_wait(barrier, n - 1 + tn - 1)

    def rotate(u):
        return u * cosine[...] + pltpu.roll(u, half, 1) * sine[...]

    def rounded(u):
        return u.astype(bf16).astype(f32)

    def send(kind, r, source, target):
        return pltpu.make_async_remote_copy(
            src_ref=source, dst_ref=target, send_sem=s_sem.at[kind, r - 1],
            recv_sem=r_sem.at[kind, r - 1], device_id={"ctx": peers[r - 1]}, device_id_type=MESH)

    mine = lax.rem(me, owners)
    my_kv = (mine * hpo) // group
    rows = hpo * batch
    my_rows = pl.ds(pl.multiple_of(me * rows, rows), rows)
    width = hpo * hd

    def layer_step(l, carry):
        stream = out_ref[...]
        scaled = (stream * gain[l]).astype(bf16)
        squares = stream * stream
        fold = squares[:, 0:hd]
        for c in range(1, feat // hd):
            fold = fold + squares[:, c * hd:(c + 1) * hd]
        load(0, l).wait()

        @pl.when(l + 1 < layers)
        def _():
            for index in range(len(weights)):
                load(index, l + 1).start()

        q = jnp.dot(scaled, wq[l], preferred_element_type=f32)
        for i in range(owners):
            qp[i, :, 0:width] = q[:, i * width:(i + 1) * width]
            qp[i, :, width:width + hd] = fold
        qs = []
        for r in range(1, n):
            c = send(0, r, qp.at[lax.rem(peers[r - 1], owners)], qr.at[r - 1])
            c.start()
            qs.append(c)
        load(1, l).wait()
        load(2, l).wait()
        k = jnp.dot(scaled, wk[l], preferred_element_type=f32)
        v = jnp.dot(scaled, wv[l], preferred_element_type=f32)
        for j in range(kvl):
            kvp[j, :, 0:hd] = k[:, j * hd:(j + 1) * hd]
            kvp[j, :, hd:2 * hd] = v[:, j * hd:(j + 1) * hd]
        ks = []
        for r in range(1, n):
            owner = lax.rem(peers[r - 1], owners)
            c = send(1, r, kvp.at[(owner * hpo) // group], kvr.at[r - 1])
            c.start()
            ks.append(c)
        for c in qs:
            c.wait_recv()
        whole = qp[mine]
        for r in range(1, n):
            whole = whole + qr[r - 1]
        inverse = lax.rsqrt(jnp.sum(whole[:, width:width + hd], axis=1, keepdims=True) / total + norm_eps)
        for t in range(hpo):
            u = rotate(whole[:, t * hd:(t + 1) * hd] * inverse)
            qown[t] = rounded(u)
            qf[pl.ds(pl.multiple_of(me * rows + t * batch, batch), batch), :] = u
        gs = []
        for r in range(1, n):
            c = send(2, r, qf.at[my_rows], qf.at[my_rows])
            c.start()
            gs.append(c)
        for c in ks:
            c.wait_recv()
        kv = kvp[my_kv]
        for r in range(1, n):
            kv = kv + kvr[r - 1]
        new_key = rounded(rotate(kv[:, 0:hd] * inverse))
        new_value = rounded(kv[:, hd:2 * hd] * inverse)
        own = [jnp.sum(qown[t] * new_key, axis=1, keepdims=True) * scale for t in range(hpo)]
        load(3, l).wait()
        load(4, l).wait()
        for c in gs:
            c.wait_recv()
        scores = []
        for b in range(batch):
            qb = qf[pl.ds(b, heads, stride=batch), :].astype(bf16)
            for j in range(kvl):
                scores.append(lax.dot_general(
                    qb[j * group:(j + 1) * group], kc[l, b, j], (((1,), (1,)), ((), ())),
                    preferred_element_type=f32))
        masked = jnp.concatenate(scores, axis=0) * scale + bias[...]
        top = jnp.max(masked, axis=1, keepdims=True)
        weight = jnp.exp(masked - top)
        weight_sum = jnp.sum(weight, axis=1, keepdims=True)
        narrow = weight.astype(bf16)
        lanes = lax.broadcasted_iota(jnp.int32, (batch * heads, hd), 1)
        stmp[...] = jnp.where(lax.rem(lanes, 2) == 0, top, weight_sum)
        for b in range(batch):
            for j in range(kvl):
                at = b * heads + j * group
                otmp[at:at + group, :] = jnp.dot(narrow[at:at + group], vc[l, b, j], preferred_element_type=f32)
        for c in qs + ks + gs:
            c.wait_send()
        for i in range(owners):
            stat = None
            for t in range(hpo):
                h = i * hpo + t
                op[i, t * batch:(t + 1) * batch, :] = otmp[pl.ds(h, batch, stride=heads), :]
                piece = stmp[pl.ds(h, batch, stride=heads), :]
                stat = piece if stat is None else jnp.where(lane < 2 * t, stat, piece)
            op[i, rows:rows + batch, :] = stat
        os_ = []
        for r in range(1, n):
            c = send(3, r, op.at[lax.rem(peers[r - 1], owners)], orr.at[r - 1])
            c.start()
            os_.append(c)
        for c in os_:
            c.wait_recv()
        parts = [op[mine]] + [orr[r - 1] for r in range(1, n)]
        for t in range(hpo):
            tops = [part[rows:rows + batch, 2 * t:2 * t + 1] for part in parts]
            sums = [part[rows:rows + batch, 2 * t + 1:2 * t + 2] for part in parts]
            largest = own[t]
            for x in tops:
                largest = jnp.maximum(largest, x)
            fresh = jnp.exp(own[t] - largest)
            numerator = rounded(fresh) * new_value
            denominator = fresh
            for x, s, part in zip(tops, sums, parts):
                factor = jnp.exp(x - largest)
                denominator = denominator + s * factor
                numerator = numerator + part[t * batch:(t + 1) * batch, :] * factor
            cf[pl.ds(pl.multiple_of(me, 1), 1), :, t * hd:(t + 1) * hd] = (numerator / denominator)[None]
        cs = []
        for r in range(1, n):
            c = send(4, r, cf.at[me], cf.at[me])
            c.start()
            cs.append(c)
        load(5, l).wait()
        for c in cs:
            c.wait_recv()
        context = jnp.concatenate([cf[i] for i in range(owners)], axis=1).astype(bf16)
        part = jnp.dot(context, wo[l], preferred_element_type=f32)
        odd = lax.rem(l, 2)
        tps[...] = part
        ts = []
        for r in range(1, tn):
            c = pltpu.make_async_remote_copy(
                src_ref=tps, dst_ref=tpr.at[odd, r - 1], send_sem=ts_sem.at[r - 1],
                recv_sem=tr_sem.at[odd, r - 1], device_id={"tp": tpeers[r - 1]}, device_id_type=MESH)
            c.start()
            ts.append(c)
        for c in os_ + cs:
            c.wait_send()
        stream = stream + part
        for r, c in enumerate(ts):
            c.wait_recv()
            stream = stream + tpr[odd, r]
        out_ref[...] = stream
        for c in ts:
            c.wait_send()
        return carry

    lax.fori_loop(0, layers, layer_step, 0)


def shards(sizes, hidden, norm_gains, w_query, w_key, w_value, w_out, key_cache, value_cache, lengths):
    n, tn = sizes
    layers, feat, columns = w_query.shape
    batch = hidden.shape[0]
    _, _, kvl, span, hd = key_cache.shape
    heads = columns // hd
    hpo = max(1, heads // n)
    owners = heads // hpo
    dims = (n, tn, layers, batch, feat, feat * n, heads, kvl, hd, span)
    f32 = jnp.float32
    vmem = pl.BlockSpec(memory_space=pltpu.VMEM)
    far = pl.BlockSpec(memory_space=pl.ANY)

    def like(array):
        return pltpu.VMEM(array.shape, array.dtype)

    return pl.pallas_call(
        functools.partial(kernel, dims),
        out_shape=jax.ShapeDtypeStruct((batch, feat), f32),
        in_specs=[vmem, vmem, pl.BlockSpec(memory_space=pltpu.SMEM)] + [far] * 6,
        out_specs=vmem,
        scratch_shapes=[
            like(w_query), like(w_key), like(w_value), like(w_out), like(key_cache), like(value_cache),
            pltpu.VMEM((layers, batch, feat), f32),
            pltpu.VMEM((batch * heads, span), f32),
            pltpu.VMEM((batch, hd), f32),
            pltpu.VMEM((batch, hd), f32),
            pltpu.VMEM((owners, batch, hpo * hd + hd), f32),
            pltpu.VMEM((n - 1, batch, hpo * hd + hd), f32),
            pltpu.VMEM((kvl, batch, 2 * hd), f32),
            pltpu.VMEM((n - 1, batch, 2 * hd), f32),
            pltpu.VMEM((n * hpo * batch, hd), f32),
            pltpu.VMEM((hpo, batch, hd), f32),
            pltpu.VMEM((batch * heads, hd), f32),
            pltpu.VMEM((batch * heads, hd), f32),
            pltpu.VMEM((owners, hpo * batch + batch, hd), f32),
            pltpu.VMEM((n - 1, hpo * batch + batch, hd), f32),
            pltpu.VMEM((n, batch, hpo * hd), f32),
            pltpu.VMEM((batch, feat), f32),
            pltpu.VMEM((2, tn - 1, batch, feat), f32),
            pltpu.SemaphoreType.DMA((6, layers)),
            pltpu.SemaphoreType.DMA((5, n - 1)),
            pltpu.SemaphoreType.DMA((5, n - 1)),
            pltpu.SemaphoreType.DMA((tn - 1,)),
            pltpu.SemaphoreType.DMA((2, tn - 1)),
        ],
        compiler_params=pltpu.CompilerParams(
            collective_id=0, has_side_effects=True, vmem_limit_bytes=60 * 1024 * 1024),
    )(hidden, norm_gains, lengths, w_query, w_key, w_value, w_out, key_cache, value_cache)


def solution(mesh):
    sizes = (mesh.shape["ctx"], mesh.shape["tp"])
    return jax.shard_map(
        functools.partial(shards, sizes),
        mesh=mesh,
        in_specs=(
            P(None, "ctx"),
            P(None, "ctx"),
            P(None, "ctx", "tp"),
            P(None, "ctx", "tp"),
            P(None, "ctx", "tp"),
            P(None, "tp", "ctx"),
            P(None, None, "tp", "ctx", None),
            P(None, None, "tp", "ctx", None),
            P(),
        ),
        out_specs=P(None, "ctx"),
        check_vma=False,
    )
```

time: 527 us -> 90.2 us (0.17)
  blocking collectives: 275 us -> 0 us
  waiting for transfers between devices: 179 us -> 0 us
  Pallas kernels: 0 us -> 88.6 us
  matrix products: 43.4 us -> 0 us
  between operations: 13.6 us -> 0.01 us
  other arithmetic: 12 us -> 0 us
    psum x4 -> x0, waiting for transfers between devices: 179 us -> none  [shards(): lax.psum((query_part, key_part, value_part), 'ctx')]
    psum x8 -> x0, blocking collectives: 169 us -> none  [the longest x4 92.6 us: shards(): squares = lax.psum(local_squares, 'ctx')]
    all_gather x12 -> x0, blocking collectives: 106 us -> none  [merged(): pieces = jax.tree.map(lambda part: lax.all_gather(part, axis), value)]
    pallas_call x0 -> x1, Pallas kernels: none -> 88.6 us  [shards(): pl.pallas_call(functools.partial(kernel, dims), out_shape=jax.ShapeDtypeS...]
    dot_general x28 -> x0, matrix products: 43.4 us -> none  [the longest x4 14 us: shards(): jnp.dot(scaled, w_query[layer_idx], preferred_element_type=jnp.float32)]
  transfers between devices with their start and end apart: 4 -> 0, of which waited for: 4 -> 0; matrix products, arithmetic and copies ran while one was open for 0% -> 0% of each run, Pallas kernels for 0% -> 0%
where the time goes in v1:
time: 90.2 us; the launch traced here: 90 us
  Pallas kernels  88.6 us (98%)
  local copies, waits for them, and re-layouts  1.38 us (2%)
    pallas_call x1, Pallas kernels, shards(): pl.pallas_call(functools.partial(kernel, dims), out_shape=jax.ShapeDtypeS...  88.6 us

profile of v1, /device:TPU:0, one launch (start us, length us, event | category | flops | bytes accessed | tf_op | source)
XLA Modules:
  0.0 90.0 jit_solution(10763424506979323284)
XLA Ops:
  0.0 88.6 %shard_map.91 = f32[8,1024]{1,0:T(8,128)} custom-call(bf16[8,1024]{1,0:T(8,128)(2,1)} %hidden_ref.1, bf16[4,1024]{1,0:T(4,128)(2,1)} %gains_ref.1, s32[8]{0:T(128)} %lengths_ref.1, bf16[4,1024,2048]{2,1,0:T(8,128)(2,1)} %wq_h.1, bf16[4,1024,256]{2,1,0:T(8,128)(2,1)} %wk_h.1, bf16[4,1024,256]{2,1,0:T(8,128)(2,1)} %wv_h.1, bf16[4,2048,1024]{2,1,0:T(8,128)(2,1)} %wo_h.1, ...), custom_call_target="tpu_custom_call" | custom-call | tf_op jit(solution)/shard_map/pallas_call | solution.py:243
  88.6 1.4 %copy.11 = f32[8,1024]{1,0:T(8,128)} copy(f32[8,1024]{1,0:T(8,128)} %shard_map.91) | data formatting | bytes 65536

commit v2 on v1

--- a/solution.py
+++ b/solution.py
@@ -22,6 +22,8 @@
     hpo = max(1, heads // n)
     owners = heads // hpo
     f32, bf16 = jnp.float32, jnp.bfloat16
+    pieces = tps.shape[0]
+    piece = feat // pieces
     scale = 1.0 / math.sqrt(hd)
     me = lax.axis_index("ctx")
     mt = lax.axis_index("tp")
@@ -72,6 +74,7 @@
             src_ref=source, dst_ref=target, send_sem=s_sem.at[kind, r - 1],
             recv_sem=r_sem.at[kind, r - 1], device_id={"ctx": peers[r - 1]}, device_id_type=MESH)
 
+    order = sorted(range(1, n), key=lambda r: (-min(r, n - r), r))
     mine = lax.rem(me, owners)
     my_kv = (mine * hpo) // group
     rows = hpo * batch
@@ -97,7 +100,7 @@
             qp[i, :, 0:width] = q[:, i * width:(i + 1) * width]
             qp[i, :, width:width + hd] = fold
         qs = []
-        for r in range(1, n):
+        for r in order:
             c = send(0, r, qp.at[lax.rem(peers[r - 1], owners)], qr.at[r - 1])
             c.start()
             qs.append(c)
@@ -109,7 +112,7 @@
             kvp[j, :, 0:hd] = k[:, j * hd:(j + 1) * hd]
             kvp[j, :, hd:2 * hd] = v[:, j * hd:(j + 1) * hd]
         ks = []
-        for r in range(1, n):
+        for r in order:
             owner = lax.rem(peers[r - 1], owners)
             c = send(1, r, kvp.at[(owner * hpo) // group], kvr.at[r - 1])
             c.start()
@@ -125,7 +128,7 @@
             qown[t] = rounded(u)
             qf[pl.ds(pl.multiple_of(me * rows + t * batch, batch), batch), :] = u
         gs = []
-        for r in range(1, n):
+        for r in order:
             c = send(2, r, qf.at[my_rows], qf.at[my_rows])
             c.start()
             gs.append(c)
@@ -166,11 +169,11 @@
             for t in range(hpo):
                 h = i * hpo + t
                 op[i, t * batch:(t + 1) * batch, :] = otmp[pl.ds(h, batch, stride=heads), :]
-                piece = stmp[pl.ds(h, batch, stride=heads), :]
-                stat = piece if stat is None else jnp.where(lane < 2 * t, stat, piece)
+                tile = stmp[pl.ds(h, batch, stride=heads), :]
+                stat = tile if stat is None else jnp.where(lane < 2 * t, stat, tile)
             op[i, rows:rows + batch, :] = stat
         os_ = []
-        for r in range(1, n):
+        for r in order:
             c = send(3, r, op.at[lax.rem(peers[r - 1], owners)], orr.at[r - 1])
             c.start()
             os_.append(c)
@@ -192,7 +195,7 @@
                 numerator = numerator + part[t * batch:(t + 1) * batch, :] * factor
             cf[pl.ds(pl.multiple_of(me, 1), 1), :, t * hd:(t + 1) * hd] = (numerator / denominator)[None]
         cs = []
-        for r in range(1, n):
+        for r in order:
             c = send(4, r, cf.at[me], cf.at[me])
             c.start()
             cs.append(c)
@@ -200,23 +203,26 @@
         for c in cs:
             c.wait_recv()
         context = jnp.concatenate([cf[i] for i in range(owners)], axis=1).astype(bf16)
-        part = jnp.dot(context, wo[l], preferred_element_type=f32)
         odd = lax.rem(l, 2)
-        tps[...] = part
         ts = []
-        for r in range(1, tn):
-            c = pltpu.make_async_remote_copy(
-                src_ref=tps, dst_ref=tpr.at[odd, r - 1], send_sem=ts_sem.at[r - 1],
-                recv_sem=tr_sem.at[odd, r - 1], device_id={"tp": tpeers[r - 1]}, device_id_type=MESH)
-            c.start()
-            ts.append(c)
+        for g in range(pieces):
+            cut = slice(g * piece, (g + 1) * piece)
+            tps[g] = jnp.dot(context, wo[l, :, cut], preferred_element_type=f32)
+            for r in range(1, tn):
+                c = pltpu.make_async_remote_copy(
+                    src_ref=tps.at[g], dst_ref=tpr.at[odd, g, r - 1], send_sem=ts_sem.at[g, r - 1],
+                    recv_sem=tr_sem.at[odd, g, r - 1], device_id={"tp": tpeers[r - 1]}, device_id_type=MESH)
+                c.start()
+                ts.append(c)
         for c in os_ + cs:
             c.wait_send()
-        stream = stream + part
-        for r, c in enumerate(ts):
-            c.wait_recv()
-            stream = stream + tpr[odd, r]
-        out_ref[...] = stream
+        for g in range(pieces):
+            cut = slice(g * piece, (g + 1) * piece)
+            moved = out_ref[:, cut] + tps[g]
+            for r in range(1, tn):
+                ts[g * (tn - 1) + r - 1].wait_recv()
+                moved = moved + tpr[odd, g, r - 1]
+            out_ref[:, cut] = moved
         for c in ts:
             c.wait_send()
         return carry
@@ -233,6 +239,7 @@
     hpo = max(1, heads // n)
     owners = heads // hpo
     dims = (n, tn, layers, batch, feat, feat * n, heads, kvl, hd, span)
+    pieces = 2
     f32 = jnp.float32
     vmem = pl.BlockSpec(memory_space=pltpu.VMEM)
     far = pl.BlockSpec(memory_space=pl.ANY)
@@ -262,13 +269,13 @@
             pltpu.VMEM((owners, hpo * batch + batch, hd), f32),
             pltpu.VMEM((n - 1, hpo * batch + batch, hd), f32),
             pltpu.VMEM((n, batch, hpo * hd), f32),
-            pltpu.VMEM((batch, feat), f32),
-            pltpu.VMEM((2, tn - 1, batch, feat), f32),
+            pltpu.VMEM((pieces, batch, feat // pieces), f32),
+            pltpu.VMEM((2, pieces, tn - 1, batch, feat // pieces), f32),
             pltpu.SemaphoreType.DMA((6, layers)),
             pltpu.SemaphoreType.DMA((5, n - 1)),
             pltpu.SemaphoreType.DMA((5, n - 1)),
-            pltpu.SemaphoreType.DMA((tn - 1,)),
-            pltpu.SemaphoreType.DMA((2, tn - 1)),
+            pltpu.SemaphoreType.DMA((pieces, tn - 1)),
+            pltpu.SemaphoreType.DMA((2, pieces, tn - 1)),
         ],
         compiler_params=pltpu.CompilerParams(
             collective_id=0, has_side_effects=True, vmem_limit_bytes=60 * 1024 * 1024),

time: 90.2 us -> 89.7 us (level)
  no operation moved by 1% of the time
where the time goes in v2:
time: 89.7 us; the launch traced here: 89.4 us
  Pallas kernels  88 us (98%)
  local copies, waits for them, and re-layouts  1.38 us (2%)
    pallas_call x1, Pallas kernels, shards(): pl.pallas_call(functools.partial(kernel, dims), out_shape=jax.ShapeDtypeS...  88 us

profile of v2, /device:TPU:0, one launch (start us, length us, event | category | flops | bytes accessed | tf_op | source)
XLA Modules:
  0.0 89.4 jit_solution(12034133344708569807)
XLA Ops:
  0.0 88.0 %shard_map.91 = f32[8,1024]{1,0:T(8,128)} custom-call(bf16[8,1024]{1,0:T(8,128)(2,1)} %hidden_ref.1, bf16[4,1024]{1,0:T(4,128)(2,1)} %gains_ref.1, s32[8]{0:T(128)} %lengths_ref.1, bf16[4,1024,2048]{2,1,0:T(8,128)(2,1)} %wq_h.1, bf16[4,1024,256]{2,1,0:T(8,128)(2,1)} %wk_h.1, bf16[4,1024,256]{2,1,0:T(8,128)(2,1)} %wv_h.1, bf16[4,2048,1024]{2,1,0:T(8,128)(2,1)} %wo_h.1, ...), custom_call_target="tpu_custom_call" | custom-call | tf_op jit(solution)/shard_map/pallas_call | solution.py:250
  88.1 1.4 %copy.11 = f32[8,1024]{1,0:T(8,128)} copy(f32[8,1024]{1,0:T(8,128)} %shard_map.91) | data formatting | bytes 65536
